TPU v7x, 32 devices: a whole 2x2x4 slice. The times are simulated.
32 devices in a mesh: group: 8 (over y, x, core), tile: 4 (over z).
Axes of the slice: x: 2, y: 2, z: 4, core: 2. Of those that a mesh axis runs over, the one named last changes fastest.
Arguments:
- coupling: float32 [32, 1024, 768], P('group', None, 'tile'), may hold values from -6 to 6
- interior_solve: float32 [32, 768, 1024], P('group', 'tile'), may hold values from -0.21875 to 0.21875
- boundary_stiffness: float32 [32, 1024, 1024], P('group', 'tile'), may hold values from -6 to 6
- migration: int32 [32], replicated, may hold values from -1 to 15, as said below
Outputs:
- condensed: float32 [16, 1024, 1024], P('group', 'tile')
Inputs may be any that keep to these rules, and one draw needn't show every extreme that they name: `migration`: every condensed slot is named by exactly one RVE slot; RVE slots of group g are g * 4 to g * 4 + 3; the condensed slots of group g are named only by RVE slots of group g or of its partner, the group whose index differs from g in the lowest bit; some group holds 4 plastic RVEs.
All inputs are finite; a program needn't handle non-finite values.
Results may differ from a plain program's by a relative error of at most 0.000071.
Values sent between devices are 32-bit elements; how exact they have to be, the bound alone decides.
A program may use at most 64 MiB of HBM per device.

v0:
```python
import jax
import jax.numpy as jnp
from jax import lax
from jax.experimental import pallas as pl
from jax.experimental.pallas import tpu as pltpu
from jax.sharding import PartitionSpec as P

OWN = 2


def swapped(array, axis, distance):
    return lax.ppermute(array, axis, [(i, i ^ 1 << distance) for i in range(lax.axis_size(axis))])


def condense(coupling_cols, solve_rows, stiff_rows):
    product = lax.psum_scatter(
        jnp.dot(
            coupling_cols,
            solve_rows,
            precision=lax.Precision.HIGHEST,
            preferred_element_type=jnp.float32,
        ),
        "tile",
        scatter_dimension=0,
        tiled=True,
    )
    return stiff_rows - product


def select_slots(stacked, positions, present):
    chosen = jnp.take(stacked, positions, axis=0)
    shaped = present.reshape((-1,) + (1,) * (stacked.ndim - 1))
    return jnp.where(shaped, chosen, jnp.zeros_like(chosen))


def portable_body(coupling, interior_solve, boundary_stiffness, migration):
    home_count = coupling.shape[0]
    mygroup = lax.axis_index("group")
    partner = jnp.bitwise_xor(mygroup, 1)
    own_plan = lax.dynamic_slice_in_dim(migration, mygroup * home_count, home_count)
    slot_ids = jnp.arange(OWN, dtype=jnp.int32)
    local_ids = jnp.arange(home_count, dtype=jnp.int32)

    def locate(wanted):
        matches = own_plan[None, :] == wanted[:, None]
        positions = jnp.sum(jnp.where(matches, local_ids[None, :], 0), axis=1)
        return (positions, jnp.any(matches, axis=1))

    mine_index, mine_here = locate(mygroup * OWN + slot_ids)
    their_index, their_here = locate(partner * OWN + slot_ids)
    keep_mask = mine_here[:, None, None]
    outgoing = (
        select_slots(coupling, their_index, their_here),
        select_slots(interior_solve, their_index, their_here),
        select_slots(boundary_stiffness, their_index, their_here),
    )
    arrived = swapped((outgoing[0], outgoing[1], outgoing[2]), "group", 0)
    kept_coupling = jnp.where(keep_mask, jnp.take(coupling, mine_index, axis=0), arrived[0])
    kept_solve = jnp.where(keep_mask, jnp.take(interior_solve, mine_index, axis=0), arrived[1])
    kept_stiff = jnp.where(keep_mask, jnp.take(boundary_stiffness, mine_index, axis=0), arrived[2])
    result = jnp.stack(
        [condense(kept_coupling[slot], kept_solve[slot], kept_stiff[slot]) for slot in range(OWN)]
    )
    return result


MESH = pl.DeviceIdType.MESH
LINE = 4
CHUNKS = 8
STRIP = 16


def split_into(stack, slot, base, depth, rows, cols, value, order):
    high = value.astype(jnp.bfloat16)
    low = (value - high.astype(jnp.float32)).astype(jnp.bfloat16)
    for place, term in enumerate(order):
        at = pl.ds(base + place * depth + rows, value.shape[0])
        stack[slot, at, cols] = high if term == 0 else low


def contract(left, right):
    return lax.dot_general(left, right, (((0,), (0,)), ((), ())), preferred_element_type=jnp.float32)


def line_kernel(
    plan, k_hbm, x_hbm, b_hbm, result,
    k_home, x_home, b_home, k_out, x_out, b_out, k_in, x_in, b_in, k_got, x_got,
    k_end, x_end, k_stack, x_stack, p_send, p_recv, e_send, e_recv,
    load_sem, mig_send, mig_recv, em_send, em_recv, mm_send, mm_recv, me_send, me_recv, turn_sem,
):
    home, depth, columns = x_home.shape
    rows = b_home.shape[1]
    width = columns // CHUNKS
    last = LINE - 1
    g, t = lax.axis_index("group"), lax.axis_index("tile")
    partner = g + 1 - 2 * (g % 2)
    middle = (t % last + last - 1) // last
    is_end = middle == 0
    is_mid = middle == 1
    mid = 1 + t // last
    end = (t - 1) * last
    across = last - t
    far_end_of_end = last - t
    far_mid_of_end = last - mid
    far_end_of_mid = (2 - t) * last

    def block(index):
        return pl.ds(pl.multiple_of(index * rows, rows), rows)

    def chunk(index):
        return pl.ds(pl.multiple_of(index * width, width), width)

    loads = [
        pltpu.make_async_copy(src, dst, load_sem.at[i])
        for i, (src, dst) in enumerate(((k_hbm, k_home), (x_hbm, x_home), (b_hbm, b_home)))
    ]
    loads[0].start()
    loads[1].start()

    barrier = pltpu.get_barrier_semaphore()
    pl.semaphore_signal(barrier, inc=1, device_id=(partner, t), device_id_type=MESH)

    @pl.when(is_end)
    def _():
        pl.semaphore_signal(barrier, inc=1, device_id=(g, mid), device_id_type=MESH)

    @pl.when(is_mid)
    def _():
        pl.semaphore_signal(barrier, inc=1, device_id=(g, end), device_id_type=MESH)
        pl.semaphore_signal(barrier, inc=1, device_id=(g, across), device_id_type=MESH)

    def find(wanted):
        index, here = jnp.int32(0), jnp.int32(0)
        for j in range(home):
            hit = plan[g * home + j] == wanted
            index, here = jnp.where(hit, j, index), jnp.where(hit, 1, here)
        return index, here > 0

    mine = [find(g * OWN + s) for s in range(OWN)]
    theirs = [find(partner * OWN + s) for s in range(OWN)]

    def migrate(s, kind):
        src, dst = ((k_out, k_in), (x_out, x_in), (b_out, b_in))[kind]
        return pltpu.make_async_remote_copy(
            src_ref=src.at[s], dst_ref=dst.at[s], send_sem=mig_send.at[s, kind], recv_sem=mig_recv.at[s, kind],
            device_id=(partner, t), device_id_type=MESH,
        )

    def gather(src, dst, count):
        for s in range(OWN):
            @pl.loop(0, count // STRIP)
            def _(i):
                at = pl.ds(pl.multiple_of(i * STRIP, STRIP), STRIP)
                dst[s, at, :] = src[theirs[s][0], at, :]

    loads[0].wait()
    gather(k_home, k_out, depth)
    loads[1].wait()
    gather(x_home, x_out, depth)

    @pl.when(is_end)
    def _():
        pl.semaphore_wait(barrier, 2)

    @pl.when(is_mid)
    def _():
        pl.semaphore_wait(barrier, 3)

    for s in range(OWN):
        for kind in range(2):
            migrate(s, kind).start()
    loads[2].start()

    def settle(s, kind):
        migrate(s, kind).wait_recv()
        index, here = mine[s]
        got, own, arrived = ((k_got, k_home, k_in), (x_got, x_home, x_in))[kind]

        @pl.loop(0, depth // STRIP)
        def _(i):
            at = pl.ds(pl.multiple_of(i * STRIP, STRIP), STRIP)
            got[s, at, :] = jnp.where(here, own[index, at, :], arrived[s, at, :])

    def stack_own(s):
        @pl.loop(0, depth // STRIP)
        def _(i):
            first = pl.multiple_of(i * STRIP, STRIP)
            at = pl.ds(first, STRIP)
            everything = slice(None)
            split_into(k_stack, s, 0, depth, first, everything, k_got[s, at, :], (0, 0, 1))
            split_into(x_stack, s, 0, depth, first, everything, x_got[s, at, :], (0, 1, 0))

    def send_stiffness():
        loads[2].wait()
        gather(b_home, b_out, rows)
        for s in range(OWN):
            migrate(s, 2).start()

    def stiffness(s, c):
        index, here = mine[s]
        return jnp.where(here, b_home[index, :, chunk(c)], b_in[s, :, chunk(c)])

    def feed_k(s, j):
        target = (far_end_of_end, far_mid_of_end, mid)[j]
        return pltpu.make_async_remote_copy(
            src_ref=k_got.at[s, :, block(target)], dst_ref=k_end.at[s, j],
            send_sem=em_send.at[s, j], recv_sem=em_recv.at[s, j], device_id=(g, mid), device_id_type=MESH,
        )

    def feed_x(s, c):
        return pltpu.make_async_remote_copy(
            src_ref=x_got.at[s, :, chunk(c)], dst_ref=x_end.at[s, :, chunk(c)],
            send_sem=em_send.at[s, last + c], recv_sem=em_recv.at[s, last + c],
            device_id=(g, mid), device_id_type=MESH,
        )

    def cross(s, j, c):
        return pltpu.make_async_remote_copy(
            src_ref=p_send.at[s, j, c], dst_ref=p_recv.at[s, j, c],
            send_sem=mm_send.at[s, j, c], recv_sem=mm_recv.at[s, j, c],
            device_id=(g, across), device_id_type=MESH,
        )

    def deliver(s, c):
        return pltpu.make_async_remote_copy(
            src_ref=e_send.at[s, c], dst_ref=e_recv.at[s, c],
            send_sem=me_send.at[s, c], recv_sem=me_recv.at[s, c],
            device_id=(g, end), device_id_type=MESH,
        )

    own_terms = pl.ds(0, 3 * depth)

    @pl.when(is_end)
    def _():
        for s in range(OWN):
            settle(s, 0)
            if s == 0:
                @pl.when(g % 2 == 1)
                def _():
                    pl.semaphore_wait(turn_sem, 1)

            feed_k(s, 0).start()
            settle(s, 1)
            for c in range(CHUNKS):
                feed_x(s, c).start()
            feed_k(s, 1).start()
            if s == 0:
                @pl.when(g % 2 == 0)
                def _():
                    feed_k(0, 1).wait_send()
                    pl.semaphore_signal(turn_sem, inc=1, device_id=(partner, t), device_id_type=MESH)

            feed_k(s, 2).start()
        send_stiffness()
        for s in range(OWN):
            stack_own(s)
        for s in range(OWN):
            migrate(s, 2).wait_recv()

            @pl.loop(0, CHUNKS)
            def _(c):
                result[s, :, chunk(c)] = stiffness(s, c) - contract(
                    k_stack[s, own_terms, block(t)], x_stack[s, own_terms, chunk(c)]
                )

        for s in range(OWN):
            @pl.loop(0, CHUNKS)
            def _(c):
                pltpu.make_async_remote_copy(
                    src_ref=e_send.at[s, c], dst_ref=e_recv.at[s, c],
                    send_sem=me_send.at[s, c], recv_sem=me_recv.at[s, c],
                    device_id=(g, mid), device_id_type=MESH,
                ).wait_recv()
                result[s, :, chunk(c)] = result[s, :, chunk(c)] - e_recv[s, c]

        @pl.when(g % 2 == 1)
        def _():
            feed_k(0, 1).wait_send()

        for s in range(OWN):
            feed_k(s, 0).wait_send()
            if s > 0:
                feed_k(s, 1).wait_send()
            feed_k(s, 2).wait_send()
            for c in range(CHUNKS):
                feed_x(s, c).wait_send()

    @pl.when(is_mid)
    def _():
        def arrive_k(s, j, target):
            pltpu.make_async_remote_copy(
                src_ref=k_end.at[s, j], dst_ref=k_end.at[s, j],
                send_sem=em_send.at[s, j], recv_sem=em_recv.at[s, j], device_id=(g, end), device_id_type=MESH,
            ).wait_recv()

            @pl.loop(0, depth // STRIP)
            def _(i):
                first = pl.multiple_of(i * STRIP, STRIP)
                split_into(
                    k_stack, s, 3 * depth, depth, first, block(target), k_end[s, j, pl.ds(first, STRIP), :], (0, 0, 1)
                )

        def arrive_x(s, c):
            pltpu.make_async_remote_copy(
                src_ref=x_end.at[s, :, chunk(c)], dst_ref=x_end.at[s, :, chunk(c)],
                send_sem=em_send.at[s, last + c], recv_sem=em_recv.at[s, last + c],
                device_id=(g, end), device_id_type=MESH,
            ).wait_recv()

            @pl.loop(0, depth // STRIP)
            def _(i):
                first = pl.multiple_of(i * STRIP, STRIP)
                split_into(
                    x_stack, s, 3 * depth, depth, first, chunk(c), x_end[s, pl.ds(first, STRIP), chunk(c)], (0, 1, 0)
                )

        def produce(s):
            arrive_k(s, 0, far_end_of_mid)

            @pl.loop(0, CHUNKS)
            def _(c):
                arrive_x(s, c)
                p_send[s, 0, c] = contract(k_stack[s, :, block(far_end_of_mid)], x_stack[s, :, chunk(c)])
                cross(s, 0, c).start()

            arrive_k(s, 1, across)

            @pl.loop(0, CHUNKS)
            def _(c):
                p_send[s, 1, c] = contract(k_stack[s, :, block(across)], x_stack[s, :, chunk(c)])
                cross(s, 1, c).start()

        def forward(s):
            @pl.loop(0, CHUNKS)
            def _(c):
                part = contract(k_stack[s, own_terms, block(end)], x_stack[s, own_terms, chunk(c)])
                cross(s, 0, c).wait_recv()
                e_send[s, c] = p_recv[s, 0, c] + part
                deliver(s, c).start()

        def own_share(s):
            arrive_k(s, 2, t)
            migrate(s, 2).wait_recv()

            @pl.loop(0, CHUNKS)
            def _(c):
                result[s, :, chunk(c)] = stiffness(s, c) - contract(k_stack[s, :, block(t)], x_stack[s, :, chunk(c)])

        def finish(s):
            @pl.loop(0, CHUNKS)
            def _(c):
                cross(s, 1, c).wait_recv()
                result[s, :, chunk(c)] = result[s, :, chunk(c)] - p_recv[s, 1, c]

        for s in range(OWN):
            settle(s, 0)
            settle(s, 1)
            stack_own(s)
        produce(0)
        send_stiffness()
        forward(0)
        produce(1)
        own_share(0)
        own_share(1)
        finish(0)
        forward(1)
        finish(1)
        for s in range(OWN):
            for c in range(CHUNKS):
                cross(s, 0, c).wait_send()
                cross(s, 1, c).wait_send()
                deliver(s, c).wait_send()

    for s in range(OWN):
        for kind in range(3):
            migrate(s, kind).wait_send()


def line_body(coupling, interior_solve, boundary_stiffness, migration):
    home, depth, columns = interior_solve.shape
    rows = boundary_stiffness.shape[1]
    width = columns // CHUNKS
    f32, bf16 = jnp.float32, jnp.bfloat16
    share = (OWN, depth, columns)
    pieces = (OWN, CHUNKS, rows, width)
    dma = pltpu.SemaphoreType.DMA
    return pl.pallas_call(
        line_kernel,
        out_shape=pltpu.VMEM((OWN, rows, columns), f32),
        in_specs=[pl.BlockSpec(memory_space=pltpu.SMEM)] + [pl.BlockSpec(memory_space=pl.ANY)] * 3,
        out_specs=pl.BlockSpec(memory_space=pltpu.VMEM),
        scratch_shapes=[
            pltpu.VMEM((home, depth, columns), f32),
            pltpu.VMEM((home, depth, columns), f32),
            pltpu.VMEM((home, rows, columns), f32),
            pltpu.VMEM(share, f32),
            pltpu.VMEM(share, f32),
            pltpu.VMEM((OWN, rows, columns), f32),
            pltpu.VMEM(share, f32),
            pltpu.VMEM(share, f32),
            pltpu.VMEM((OWN, rows, columns), f32),
            pltpu.VMEM(share, f32),
            pltpu.VMEM(share, f32),
            pltpu.VMEM((OWN, LINE - 1, depth, rows), f32),
            pltpu.VMEM(share, f32),
            pltpu.VMEM((OWN, 6 * depth, columns), bf16),
            pltpu.VMEM((OWN, 6 * depth, columns), bf16),
            pltpu.VMEM((OWN, 2, CHUNKS, rows, width), f32),
            pltpu.VMEM((OWN, 2, CHUNKS, rows, width), f32),
            pltpu.VMEM(pieces, f32),
            pltpu.VMEM(pieces, f32),
            dma((3,)),
            dma((OWN, 3)),
            dma((OWN, 3)),
            dma((OWN, LINE - 1 + CHUNKS)),
            dma((OWN, LINE - 1 + CHUNKS)),
            dma((OWN, 2, CHUNKS)),
            dma((OWN, 2, CHUNKS)),
            dma((OWN, CHUNKS)),
            dma((OWN, CHUNKS)),
            pltpu.SemaphoreType.REGULAR,
        ],
        compiler_params=pltpu.CompilerParams(
            collective_id=0, has_side_effects=True, vmem_limit_bytes=60 * 1024 * 1024
        ),
    )(migration, jnp.swapaxes(coupling, 1, 2), interior_solve, boundary_stiffness)


def solution(mesh):
    return jax.shard_map(
        line_body if mesh.shape["tile"] == LINE else portable_body,
        mesh=mesh,
        in_specs=(
            P("group", None, "tile"),
            P("group", "tile", None),
            P("group", "tile", None),
            P(),
        ),
        out_specs=P("group", "tile", None),
        check_vma=False,
    )
```

profile of v0, /device:TPU:9, one launch (start us, length us, event | category | flops | bytes accessed | tf_op | source)
XLA Modules:
  0.0 108.0 jit_solution(11532840025713463685)
XLA Ops:
  0.0 106.7 %shard_map.46 = f32[2,256,1024]{2,1,0:T(8,128)S(1)} custom-call(s32[32]{0:T(128)} %plan.1, f32[4,192,1024]{2,1,0:T(8,128)} %bitcast.1, f32[4,192,1024]{2,1,0:T(8,128)} %x_hbm.1, f32[4,256,1024]{2,1,0:T(8,128)} %b_hbm.1), custom_call_target="tpu_custom_call" | custom-call | tf_op jit(solution)/shard_map/pallas_call | solution.py:387
  106.7 1.3 %copy.6 = f32[2,256,1024]{2,1,0:T(8,128)} copy(f32[2,256,1024]{2,1,0:T(8,128)S(1)} %shard_map.46) | data formatting | bytes 4194304
where the time goes:
time: 108 us
  Pallas kernels  107 us (99%)
  local copies, waits for them, and re-layouts  1.32 us (1%)
    pallas_call x1, Pallas kernels, line_body(): pl.pallas_call(line_kernel, out_shape=pltpu.VMEM((OWN, rows, columns), f3...  107 us

commit v1 on v0

v1 whole, which is shorter than its diff:
```python
import jax
import jax.numpy as jnp
from jax import lax
from jax.experimental import pallas as pl
from jax.experimental.pallas import tpu as pltpu
from jax.sharding import PartitionSpec as P

OWN = 2


def swapped(array, axis, distance):
    return lax.ppermute(array, axis, [(i, i ^ 1 << distance) for i in range(lax.axis_size(axis))])


def condense(coupling_cols, solve_rows, stiff_rows):
    product = lax.psum_scatter(
        jnp.dot(
            coupling_cols,
            solve_rows,
            precision=lax.Precision.HIGHEST,
            preferred_element_type=jnp.float32,
        ),
        "tile",
        scatter_dimension=0,
        tiled=True,
    )
    return stiff_rows - product


def select_slots(stacked, positions, present):
    chosen = jnp.take(stacked, positions, axis=0)
    shaped = present.reshape((-1,) + (1,) * (stacked.ndim - 1))
    return jnp.where(shaped, chosen, jnp.zeros_like(chosen))


def portable_body(coupling, interior_solve, boundary_stiffness, migration):
    home_count = coupling.shape[0]
    mygroup = lax.axis_index("group")
    partner = jnp.bitwise_xor(mygroup, 1)
    own_plan = lax.dynamic_slice_in_dim(migration, mygroup * home_count, home_count)
    slot_ids = jnp.arange(OWN, dtype=jnp.int32)
    local_ids = jnp.arange(home_count, dtype=jnp.int32)

    def locate(wanted):
        matches = own_plan[None, :] == wanted[:, None]
        positions = jnp.sum(jnp.where(matches, local_ids[None, :], 0), axis=1)
        return (positions, jnp.any(matches, axis=1))

    mine_index, mine_here = locate(mygroup * OWN + slot_ids)
    their_index, their_here = locate(partner * OWN + slot_ids)
    keep_mask = mine_here[:, None, None]
    outgoing = (
        select_slots(coupling, their_index, their_here),
        select_slots(interior_solve, their_index, their_here),
        select_slots(boundary_stiffness, their_index, their_here),
    )
    arrived = swapped((outgoing[0], outgoing[1], outgoing[2]), "group", 0)
    kept_coupling = jnp.where(keep_mask, jnp.take(coupling, mine_index, axis=0), arrived[0])
    kept_solve = jnp.where(keep_mask, jnp.take(interior_solve, mine_index, axis=0), arrived[1])
    kept_stiff = jnp.where(keep_mask, jnp.take(boundary_stiffness, mine_index, axis=0), arrived[2])
    result = jnp.stack(
        [condense(kept_coupling[slot], kept_solve[slot], kept_stiff[slot]) for slot in range(OWN)]
    )
    return result


MESH = pl.DeviceIdType.MESH
LINE = 4
CHUNKS = 4
STRIP = 64
AHEAD = 3
K, X, B = 0, 1, 2
PIECES = ((K, 0), (X, 0), (K, 1), (X, 1), (X, 2), (X, 3), (K, 2), (K, 3))
FED = 7
FAR = 6


def split_into(stack, base, depth, rows, value, order):
    high = value.astype(jnp.bfloat16)
    low = (value - high.astype(jnp.float32)).astype(jnp.bfloat16)
    for place, term in enumerate(order):
        stack[pl.ds(base + place * depth + rows, value.shape[0]), :] = high if term == 0 else low


def contract(left, right):
    return lax.dot_general(left, right, (((0,), (0,)), ((), ())), preferred_element_type=jnp.float32)


def strips(count, body):
    @pl.loop(0, count // STRIP)
    def _(i):
        body(pl.multiple_of(i * STRIP, STRIP))


def line_kernel(
    plan, k_hbm, x_hbm, b_hbm, result,
    k_home0, k_home1, k_home2, k_home3, x_home0, x_home1, x_home2, x_home3, b_home,
    k_out, x_out, b_out, k_in, x_in, b_in, k_got, x_got,
    k_end, x_end, k_far, x_far, k_stack, x_stack, kf_stack, xf_stack, p_send, p_recv, e_send, e_recv,
    load_sem, mig_send, mig_recv, em_send, em_recv, far_send, far_recv, mm_send, mm_recv, me_send, me_recv,
):
    homes = ((k_home0, k_home1, k_home2, k_home3), (x_home0, x_home1, x_home2, x_home3))
    home, depth = k_home0.shape[:2]
    rows = b_home.shape[1]
    width = x_home0.shape[2]
    last = LINE - 1
    g, t = lax.axis_index("group"), lax.axis_index("tile")
    parity = g % 2
    partner = g + 1 - 2 * parity
    side = t // 2
    end, mid = side * last, 1 + side
    far_end, across = last - end, last - mid
    is_end = t == end
    is_mid = t == mid
    even_mid = is_mid & (parity == 0)
    odd_mid = is_mid & (parity == 1)

    def chunk(index):
        return pl.ds(pl.multiple_of(index * width, width), width)

    def load(q):
        kind, n = PIECES[q]
        at = chunk(n) if kind == X else pl.ds(pl.multiple_of((far_end, across, mid, end)[n] * rows, rows), rows)
        return pltpu.make_async_copy((k_hbm, x_hbm)[kind].at[:, :, at], homes[kind][n], load_sem.at[q])

    b_load = pltpu.make_async_copy(b_hbm, b_home, load_sem.at[len(PIECES)])
    for q in range(AHEAD):
        load(q).start()

    barrier = pltpu.get_barrier_semaphore()
    pl.semaphore_signal(barrier, inc=1, device_id=(partner, t), device_id_type=MESH)

    @pl.when(is_end)
    def _():
        pl.semaphore_signal(barrier, inc=1, device_id=(g, mid), device_id_type=MESH)

    @pl.when(is_mid)
    def _():
        pl.semaphore_signal(barrier, inc=1, device_id=(g, end), device_id_type=MESH)
        pl.semaphore_signal(barrier, inc=1, device_id=(g, across), device_id_type=MESH)

    def find(wanted):
        index, here = jnp.int32(0), jnp.int32(0)
        for j in range(home):
            hit = plan[g * home + j] == wanted
            index, here = jnp.where(hit, j, index), jnp.where(hit, 1, here)
        return index, here > 0

    mine = [find(g * OWN + s) for s in range(OWN)]
    theirs = [find(partner * OWN + s) for s in range(OWN)]

    def migrate(q, s):
        if q == len(PIECES):
            src, dst = b_out.at[s], b_in.at[s]
        else:
            kind, n = PIECES[q]
            src, dst = (k_out, x_out)[kind].at[s, n], (k_in, x_in)[kind].at[s, n]
        return pltpu.make_async_remote_copy(
            src_ref=src, dst_ref=dst, send_sem=mig_send.at[s, q], recv_sem=mig_recv.at[s, q],
            device_id=(partner, t), device_id_type=MESH,
        )

    def feed(s, q):
        kind, n = PIECES[q]
        return pltpu.make_async_remote_copy(
            src_ref=(k_got, x_got)[kind].at[s, n], dst_ref=(k_end, x_end)[kind].at[s, n],
            send_sem=em_send.at[s, q], recv_sem=em_recv.at[s, q], device_id=(g, mid), device_id_type=MESH,
        )

    def far(source, q):
        kind, n = PIECES[q]
        src = ((k_got, x_got), (k_end, x_end))[source][kind].at[0, n]
        return pltpu.make_async_remote_copy(
            src_ref=src, dst_ref=(k_far, x_far)[kind].at[source, n],
            send_sem=far_send.at[source, q], recv_sem=far_recv.at[source, q],
            device_id=(g, across), device_id_type=MESH,
        )

    def cross(s, j, c):
        return pltpu.make_async_remote_copy(
            src_ref=p_send.at[s, j, c], dst_ref=p_recv.at[s, j, c],
            send_sem=mm_send.at[s, j, c], recv_sem=mm_recv.at[s, j, c],
            device_id=(g, across), device_id_type=MESH,
        )

    def deliver(s, c, to):
        return pltpu.make_async_remote_copy(
            src_ref=e_send.at[s, c], dst_ref=e_recv.at[s, c],
            send_sem=me_send.at[s, c], recv_sem=me_recv.at[s, c],
            device_id=(g, to), device_id_type=MESH,
        )

    def give(q):
        kind, n = PIECES[q]
        for s in range(OWN):
            def copy(first):
                at = pl.ds(first, STRIP)
                (k_out, x_out)[kind][s, n, at, :] = homes[kind][n][theirs[s][0], at, :]

            strips(depth, copy)
            migrate(q, s).start()

    def settle(q):
        kind, n = PIECES[q]
        for s in range(OWN):
            migrate(q, s).wait_recv()
            index, here = mine[s]

            def choose(first):
                at = pl.ds(first, STRIP)
                (k_got, x_got)[kind][s, n, at, :] = jnp.where(
                    here, homes[kind][n][index, at, :], (k_in, x_in)[kind][s, n, at, :]
                )

            strips(depth, choose)
            if s == 0 and q < FED:
                @pl.when(is_end)
                def _():
                    feed(0, q).start()

            if s == 0 and q < FAR:
                @pl.when(even_mid)
                def _():
                    far(0, q).start()

    for q in range(len(PIECES)):
        load(q).wait()
        if q + AHEAD < len(PIECES):
            load(q + AHEAD).start()
        elif q + AHEAD == len(PIECES):
            b_load.start()
        if q == 0:
            @pl.when(is_end)
            def _():
                pl.semaphore_wait(barrier, 2)

            @pl.when(is_mid)
            def _():
                pl.semaphore_wait(barrier, 3)

        give(q)
        if q > 0:
            settle(q - 1)
    settle(len(PIECES) - 1)

    @pl.when(is_end)
    def _():
        for q in range(FED):
            feed(1, q).start()

    b_load.wait()
    for s in range(OWN):
        def copy(first):
            at = pl.ds(first, STRIP)
            b_out[s, at, :] = b_home[theirs[s][0], at, :]

        strips(rows, copy)
        migrate(len(PIECES), s).start()

    def stack_piece(s, kind, n):
        got, stack, order = ((k_got, k_stack, (0, 0, 1)), (x_got, x_stack, (0, 1, 0)))[kind]
        strips(depth, lambda first: split_into(
            stack.at[s, n], 0, depth, first, got[s, n, pl.ds(first, STRIP), :], order
        ))

    def stiffness(s, c):
        index, here = mine[s]
        return jnp.where(here, b_home[index, :, chunk(c)], b_in[s, :, chunk(c)])

    own_terms = pl.ds(0, 3 * depth)

    @pl.when(is_end)
    def _():
        for s in range(OWN):
            stack_piece(s, K, 3)
            for c in range(CHUNKS):
                stack_piece(s, X, c)
        for s in range(OWN):
            migrate(len(PIECES), s).wait_recv()

            @pl.loop(0, CHUNKS)
            def _(c):
                result[s, :, chunk(c)] = stiffness(s, c) - contract(k_stack[s, 3, own_terms, :], x_stack[s, c, own_terms, :])

        for s in range(OWN):
            @pl.loop(0, CHUNKS)
            def _(c):
                deliver(s, c, mid).wait_recv()
                result[s, :, chunk(c)] = result[s, :, chunk(c)] - e_recv[s, c]

        for s in range(OWN):
            for q in range(FED):
                feed(s, q).wait_send()

    def arrived(s, q):
        kind, n = PIECES[q]
        buffer = (k_end, x_end)[kind].at[s, n]
        pltpu.make_async_remote_copy(
            src_ref=buffer, dst_ref=buffer, send_sem=em_send.at[s, q], recv_sem=em_recv.at[s, q],
            device_id=(g, end), device_id_type=MESH,
        ).wait_recv()

    def stack_arrived(s, q):
        kind, n = PIECES[q]
        got, stack, order = ((k_end, k_stack, (0, 0, 1)), (x_end, x_stack, (0, 1, 0)))[kind]
        strips(depth, lambda first: split_into(
            stack.at[s, n], 3 * depth, depth, first, got[s, n, pl.ds(first, STRIP), :], order
        ))

    def stack_far(source, q):
        kind, n = PIECES[q]
        got, stack, order = ((k_far, kf_stack, (0, 0, 1)), (x_far, xf_stack, (0, 1, 0)))[kind]
        strips(depth, lambda first: split_into(
            stack.at[n], 3 * source * depth, depth, first, got[source, n, pl.ds(first, STRIP), :], order
        ))

    def produce(s):
        for q in range(FED):
            arrived(s, q)
            stack_arrived(s, q)
            kind, c = PIECES[q]
            if kind == X:
                p_send[s, 0, c] = contract(k_stack[s, 0], x_stack[s, c])
                cross(s, 0, c).start()

        @pl.loop(0, CHUNKS)
        def _(c):
            p_send[s, 1, c] = contract(k_stack[s, 1], x_stack[s, c])
            cross(s, 1, c).start()

    def forward(s):
        @pl.loop(0, CHUNKS)
        def _(c):
            part = contract(k_stack[s, 3, own_terms, :], x_stack[s, c, own_terms, :])
            cross(s, 0, c).wait_recv()
            e_send[s, c] = p_recv[s, 0, c] + part
            deliver(s, c, end).start()

    def own_share(s):
        migrate(len(PIECES), s).wait_recv()

        @pl.loop(0, CHUNKS)
        def _(c):
            result[s, :, chunk(c)] = stiffness(s, c) - contract(k_stack[s, 2], x_stack[s, c])

    def finish(s):
        @pl.loop(0, CHUNKS)
        def _(c):
            cross(s, 1, c).wait_recv()
            result[s, :, chunk(c)] = result[s, :, chunk(c)] - p_recv[s, 1, c]

    def settle_sent(s):
        for c in range(CHUNKS):
            cross(s, 0, c).wait_send()
            cross(s, 1, c).wait_send()

    @pl.when(is_mid)
    def _():
        for s in range(OWN):
            for kind, n in PIECES:
                stack_piece(s, kind, n)

    @pl.when(even_mid)
    def _():
        for q in range(FED):
            arrived(0, q)
            if q < FAR:
                far(1, q).start()
            stack_arrived(0, q)
        own_share(0)
        produce(1)
        own_share(1)
        for source in range(2):
            for q in range(FAR):
                far(source, q).wait_recv()
                stack_far(source, q)

        @pl.loop(0, CHUNKS)
        def _(c):
            e_send[0, c] = contract(k_stack[0, 3, own_terms, :], x_stack[0, c, own_terms, :]) + contract(kf_stack[0], xf_stack[c])
            deliver(0, c, end).start()

        @pl.loop(0, CHUNKS)
        def _(c):
            result[0, :, chunk(c)] = result[0, :, chunk(c)] - contract(kf_stack[1], xf_stack[c])

        forward(1)
        finish(1)
        for source in range(2):
            for q in range(FAR):
                far(source, q).wait_send()
        settle_sent(1)

    @pl.when(odd_mid)
    def _():
        produce(0)
        own_share(0)
        forward(0)
        produce(1)
        own_share(1)
        finish(0)
        forward(1)
        finish(1)
        settle_sent(0)
        settle_sent(1)

    @pl.when(is_mid)
    def _():
        for s in range(OWN):
            for c in range(CHUNKS):
                deliver(s, c, end).wait_send()

    for s in range(OWN):
        for q in range(len(PIECES) + 1):
            migrate(q, s).wait_send()


def line_body(coupling, interior_solve, boundary_stiffness, migration):
    home, depth, columns = interior_solve.shape
    rows = boundary_stiffness.shape[1]
    width = columns // CHUNKS
    f32, bf16 = jnp.float32, jnp.bfloat16
    k_share, x_share, b_share = (OWN, LINE, depth, rows), (OWN, CHUNKS, depth, width), (OWN, rows, columns)
    pieces = (OWN, CHUNKS, rows, width)
    dma = pltpu.SemaphoreType.DMA
    return pl.pallas_call(
        line_kernel,
        out_shape=pltpu.VMEM(b_share, f32),
        in_specs=[pl.BlockSpec(memory_space=pltpu.SMEM)] + [pl.BlockSpec(memory_space=pl.ANY)] * 3,
        out_specs=pl.BlockSpec(memory_space=pltpu.VMEM),
        scratch_shapes=[
            *[pltpu.VMEM((home, depth, rows), f32)] * LINE,
            *[pltpu.VMEM((home, depth, width), f32)] * CHUNKS,
            pltpu.VMEM((home, rows, columns), f32),
            pltpu.VMEM(k_share, f32),
            pltpu.VMEM(x_share, f32),
            pltpu.VMEM(b_share, f32),
            pltpu.VMEM(k_share, f32),
            pltpu.VMEM(x_share, f32),
            pltpu.VMEM(b_share, f32),
            pltpu.VMEM(k_share, f32),
            pltpu.VMEM(x_share, f32),
            pltpu.VMEM((OWN, LINE - 1, depth, rows), f32),
            pltpu.VMEM(x_share, f32),
            pltpu.VMEM((2, 2, depth, rows), f32),
            pltpu.VMEM((2, CHUNKS, depth, width), f32),
            pltpu.VMEM((OWN, LINE, 6 * depth, rows), bf16),
            pltpu.VMEM((OWN, CHUNKS, 6 * depth, width), bf16),
            pltpu.VMEM((2, 6 * depth, rows), bf16),
            pltpu.VMEM((CHUNKS, 6 * depth, width), bf16),
            pltpu.VMEM((OWN, 2, CHUNKS, rows, width), f32),
            pltpu.VMEM((OWN, 2, CHUNKS, rows, width), f32),
            pltpu.VMEM(pieces, f32),
            pltpu.VMEM(pieces, f32),
            dma((len(PIECES) + 1,)),
            dma((OWN, len(PIECES) + 1)),
            dma((OWN, len(PIECES) + 1)),
            dma((OWN, FED)),
            dma((OWN, FED)),
            dma((2, FAR)),
            dma((2, FAR)),
            dma((OWN, 2, CHUNKS)),
            dma((OWN, 2, CHUNKS)),
            dma((OWN, CHUNKS)),
            dma((OWN, CHUNKS)),
        ],
        compiler_params=pltpu.CompilerParams(
            collective_id=0, has_side_effects=True, vmem_limit_bytes=60 * 1024 * 1024
        ),
    )(migration, jnp.swapaxes(coupling, 1, 2), interior_solve, boundary_stiffness)


def solution(mesh):
    return jax.shard_map(
        line_body if mesh.shape["tile"] == LINE else portable_body,
        mesh=mesh,
        in_specs=(
            P("group", None, "tile"),
            P("group", "tile", None),
            P("group", "tile", None),
            P(),
        ),
        out_specs=P("group", "tile", None),
        check_vma=False,
    )
```

time: 108 us -> 108 us (level)
  the two profiles are of different devices: /device:TPU:9 before, /device:TPU:0 now
where the time goes in v1:
time: 108 us
  Pallas kernels  106 us (98%)
  local copies, waits for them, and re-layouts  1.32 us (1%)
    pallas_call x1, Pallas kernels, line_body(): pl.pallas_call(line_kernel, out_shape=pltpu.VMEM(b_share, f32), in_specs=...  106 us

profile of v1, /device:TPU:0, one launch (start us, length us, event | category | flops | bytes accessed | tf_op | source)
XLA Modules:
  0.0 107.8 jit_solution(8888832997909429405)
XLA Ops:
  0.0 106.5 %shard_map.46 = f32[2,256,1024]{2,1,0:T(8,128)S(1)} custom-call(s32[32]{0:T(128)} %plan.1, f32[4,192,1024]{2,1,0:T(8,128)} %bitcast.1, f32[4,192,1024]{2,1,0:T(8,128)} %x_hbm.1, f32[4,256,1024]{2,1,0:T(8,128)} %b_hbm.1), custom_call_target="tpu_custom_call" | custom-call | tf_op jit(solution)/shard_map/pallas_call | solution.py:426
  106.5 1.3 %copy.6 = f32[2,256,1024]{2,1,0:T(8,128)} copy(f32[2,256,1024]{2,1,0:T(8,128)S(1)} %shard_map.46) | data formatting | bytes 4194304

commit v2 on v1

v2 whole, which is shorter than its diff:
```python
import jax
import jax.numpy as jnp
from jax import lax
from jax.experimental import pallas as pl
from jax.experimental.pallas import tpu as pltpu
from jax.sharding import PartitionSpec as P

OWN = 2


def swapped(array, axis, distance):
    return lax.ppermute(array, axis, [(i, i ^ 1 << distance) for i in range(lax.axis_size(axis))])


def condense(coupling_cols, solve_rows, stiff_rows):
    product = lax.psum_scatter(
        jnp.dot(
            coupling_cols,
            solve_rows,
            precision=lax.Precision.HIGHEST,
            preferred_element_type=jnp.float32,
        ),
        "tile",
        scatter_dimension=0,
        tiled=True,
    )
    return stiff_rows - product


def select_slots(stacked, positions, present):
    chosen = jnp.take(stacked, positions, axis=0)
    shaped = present.reshape((-1,) + (1,) * (stacked.ndim - 1))
    return jnp.where(shaped, chosen, jnp.zeros_like(chosen))


def portable_body(coupling, interior_solve, boundary_stiffness, migration):
    home_count = coupling.shape[0]
    mygroup = lax.axis_index("group")
    partner = jnp.bitwise_xor(mygroup, 1)
    own_plan = lax.dynamic_slice_in_dim(migration, mygroup * home_count, home_count)
    slot_ids = jnp.arange(OWN, dtype=jnp.int32)
    local_ids = jnp.arange(home_count, dtype=jnp.int32)

    def locate(wanted):
        matches = own_plan[None, :] == wanted[:, None]
        positions = jnp.sum(jnp.where(matches, local_ids[None, :], 0), axis=1)
        return (positions, jnp.any(matches, axis=1))

    mine_index, mine_here = locate(mygroup * OWN + slot_ids)
    their_index, their_here = locate(partner * OWN + slot_ids)
    keep_mask = mine_here[:, None, None]
    outgoing = (
        select_slots(coupling, their_index, their_here),
        select_slots(interior_solve, their_index, their_here),
        select_slots(boundary_stiffness, their_index, their_here),
    )
    arrived = swapped((outgoing[0], outgoing[1], outgoing[2]), "group", 0)
    kept_coupling = jnp.where(keep_mask, jnp.take(coupling, mine_index, axis=0), arrived[0])
    kept_solve = jnp.where(keep_mask, jnp.take(interior_solve, mine_index, axis=0), arrived[1])
    kept_stiff = jnp.where(keep_mask, jnp.take(boundary_stiffness, mine_index, axis=0), arrived[2])
    result = jnp.stack(
        [condense(kept_coupling[slot], kept_solve[slot], kept_stiff[slot]) for slot in range(OWN)]
    )
    return result


MESH = pl.DeviceIdType.MESH
LINE = 4
CHUNKS = 4
STRIP = 64
AHEAD = 4
K, X = 0, 1
PIECES = ((K, 0), (X, 0), (K, 1), (X, 1), (X, 2), (X, 3), (K, 2), (K, 3))
K_FAR_END, K_FAR_MID, K_MID, K_END = 0, 2, 6, 7
X_AT = (1, 3, 4, 5)
UNITS = ((0, 0, 3), (0, 1, 3), (0, 2, 3)) + tuple((q, 0, 1) for q in range(1, len(PIECES)))
FED = 7
FAR = 6
LATER_FEEDS = ((0, 2), (2, 2), (4, 2), (6, 1))
LATER_CROSSES = ((0, 2), (2, 1), (3, 1))


def split_into(stack, base, depth, rows, value, order):
    high = value.astype(jnp.bfloat16)
    low = (value - high.astype(jnp.float32)).astype(jnp.bfloat16)
    for place, term in enumerate(order):
        stack[pl.ds(base + place * depth + rows, value.shape[0]), :] = high if term == 0 else low


def contract(left, right):
    return lax.dot_general(left, right, (((0,), (0,)), ((), ())), preferred_element_type=jnp.float32)


def strips(count, body):
    @pl.loop(0, count // STRIP)
    def _(i):
        body(pl.multiple_of(i * STRIP, STRIP))


def line_kernel(plan_hbm, k_hbm, x_hbm, b_hbm, result, plan, *scratch):
    homes, scratch = scratch[: len(UNITS)], scratch[len(UNITS) :]
    (
        b_home, leaving, b_out, coming, b_in, got, from_end, from_far, stack, far_stack,
        p_send, p_recv, e_send, e_recv,
        load_sem, mig_send, mig_recv, em_send, em_recv, far_send, far_recv, mm_send, mm_recv, me_send, me_recv,
    ) = scratch
    home, _, width = homes[0].shape
    depth = got.shape[2]
    rows = b_home.shape[1]
    last = LINE - 1
    g, t = lax.axis_index("group"), lax.axis_index("tile")
    parity = g % 2
    partner = g + 1 - 2 * parity
    side = t // 2
    end, mid = side * last, 1 + side
    far_end, across = last - end, last - mid
    is_end = t == end
    is_mid = t == mid
    even_mid = is_mid & (parity == 0)
    odd_mid = is_mid & (parity == 1)

    def chunk(index):
        return pl.ds(pl.multiple_of(index * width, width), width)

    def part(u):
        q, i, n = UNITS[u]
        return q, i * (depth // n), depth // n

    def load(u):
        q, first, count = part(u)
        kind, n = PIECES[q]
        at = chunk(n if kind == X else (far_end, across, mid, end)[n])
        return pltpu.make_async_copy(
            (k_hbm, x_hbm)[kind].at[:, pl.ds(first, count), at], homes[u], load_sem.at[u % AHEAD]
        )

    b_load = pltpu.make_async_copy(b_hbm, b_home, load_sem.at[AHEAD])
    plan_load = pltpu.make_async_copy(plan_hbm, plan, load_sem.at[AHEAD + 1])
    plan_load.start()
    for u in range(AHEAD):
        load(u).start()

    barrier = pltpu.get_barrier_semaphore()
    pl.semaphore_signal(barrier, inc=1, device_id=(partner, t), device_id_type=MESH)

    @pl.when(is_mid)
    def _():
        pl.semaphore_signal(barrier, inc=1, device_id=(g, across), device_id_type=MESH)
        pl.semaphore_signal(barrier, inc=1, device_id=(g, end), device_id_type=MESH)

    plan_load.wait()

    def find(wanted):
        index, here = jnp.int32(0), jnp.int32(0)
        for j in range(home):
            hit = plan[g * home + j] == wanted
            index, here = jnp.where(hit, j, index), jnp.where(hit, 1, here)
        return index, here > 0

    mine = [find(g * OWN + s) for s in range(OWN)]
    theirs = [find(partner * OWN + s) for s in range(OWN)]

    def remote(src, dst, send_sem, recv_sem, to):
        return pltpu.make_async_remote_copy(
            src_ref=src, dst_ref=dst, send_sem=send_sem, recv_sem=recv_sem, device_id=to, device_id_type=MESH
        )

    def migrate(u):
        q, first, count = part(u)
        at = pl.ds(first, count)
        return remote(leaving.at[0, q, at], coming.at[0, q, at], mig_send.at[0], mig_recv.at[u], (partner, t))

    def migrate_later():
        return remote(leaving.at[1], coming.at[1], mig_send.at[0], mig_recv.at[len(UNITS)], (partner, t))

    def migrate_b():
        return remote(b_out, b_in, mig_send.at[1], mig_recv.at[len(UNITS) + 1], (partner, t))

    def feed(q, to):
        return remote(got.at[0, q], from_end.at[0, q], em_send, em_recv.at[q], (g, to))

    def feed_later(i, to):
        at = pl.ds(*LATER_FEEDS[i])
        return remote(got.at[1, at], from_end.at[1, at], em_send, em_recv.at[FED + i], (g, to))

    def far_own(u):
        q, first, count = part(u)
        at = pl.ds(first, count)
        return remote(got.at[0, q, at], from_far.at[0, q, at], far_send, far_recv.at[0], (g, across))

    def far_end_share(q):
        return remote(from_end.at[0, q], from_far.at[1, q], far_send, far_recv.at[1 + q // 4], (g, across))

    def cross_far_end(s, c):
        return remote(
            p_send.at[s, 0, c], p_recv.at[s, 0, c], mm_send.at[s], mm_recv.at[3 + c if s else c // 2], (g, across)
        )

    def cross_far_mid(s, i):
        at = pl.ds(*LATER_CROSSES[i]) if s else pl.ds(0, CHUNKS)
        return remote(
            p_send.at[s, 1, at], p_recv.at[s, 1, at], mm_send.at[s], mm_recv.at[3 + CHUNKS + i if s else 2], (g, across)
        )

    def deliver(s, c):
        return remote(e_send.at[s, c], e_recv.at[s, c], me_send, me_recv.at[s], (g, end))

    def arrival(buffer, sem, source):
        remote(buffer, buffer, sem, sem, source).wait_recv()

    def departed(buffer, sem):
        remote(buffer, buffer, sem, sem, (partner, t)).wait_send()

    def gather(u, s):
        q, first, count = part(u)

        def copy(at):
            leaving[s, q, pl.ds(first + at, STRIP), :] = homes[u][theirs[s][0], pl.ds(at, STRIP), :]

        strips(count, copy)

    def settle(u, s):
        q, first, count = part(u)
        index, here = mine[s]

        def choose(at):
            place = pl.ds(first + at, STRIP)
            got[s, q, place, :] = jnp.where(here, homes[u][index, pl.ds(at, STRIP), :], coming[s, q, place, :])

        strips(count, choose)

    def settle_first(u):
        q, first, count = part(u)
        migrate(u).wait_recv()
        settle(u, 0)
        if q < FED and first + count == depth:
            @pl.when(is_end)
            def _():
                feed(q, mid).start()

        if q < FAR:
            @pl.when(even_mid)
            def _():
                far_own(u).start()

    for u in range(len(UNITS)):
        load(u).wait()
        if u + AHEAD < len(UNITS):
            load(u + AHEAD).start()
        elif u + AHEAD == len(UNITS):
            b_load.start()
        gather(u, 0)
        if u == 0:
            pl.semaphore_wait(barrier, 2)
        migrate(u).start()
        if u > 0:
            settle_first(u - 1)
        gather(u, 1)
    migrate_later().start()
    settle_first(len(UNITS) - 1)

    def stack_piece(s, q, source, base):
        order = ((0, 0, 1), (0, 1, 0))[PIECES[q][0]]
        strips(depth, lambda first: split_into(
            stack.at[s, q], base, depth, first, source[s, q, pl.ds(first, STRIP), :], order
        ))

    def stack_far(source, q):
        order = ((0, 0, 1), (0, 1, 0))[PIECES[q][0]]
        strips(depth, lambda first: split_into(
            far_stack.at[q], 3 * source * depth, depth, first, from_far[source, q, pl.ds(first, STRIP), :], order
        ))

    own_pieces = (K_END,) + X_AT

    @pl.when(is_mid)
    def _():
        for q in range(len(PIECES)):
            stack_piece(0, q, got, 0)

    migrate_later().wait_recv()
    for u in range(len(UNITS)):
        settle(u, 1)

    @pl.when(is_end)
    def _():
        for i in range(len(LATER_FEEDS)):
            feed_later(i, mid).start()

    @pl.when(is_mid)
    def _():
        for q in range(len(PIECES)):
            stack_piece(1, q, got, 0)

    b_load.wait()
    for s in range(OWN):
        def copy(first):
            at = pl.ds(first, STRIP)
            b_out[s, at, :] = b_home[theirs[s][0], at, :]

        strips(rows, copy)
    migrate_b().start()

    def stiffness(s, c):
        index, here = mine[s]
        return jnp.where(here, b_home[index, :, chunk(c)], b_in[s, :, chunk(c)])

    own_terms = pl.ds(0, 3 * depth)

    def x_at(c):
        return jnp.where(c == 0, X_AT[0], c + X_AT[1] - 1)

    @pl.when(is_end)
    def _():
        for s in range(OWN):
            for q in own_pieces:
                stack_piece(s, q, got, 0)
        migrate_b().wait_recv()
        for s in range(OWN):
            @pl.loop(0, CHUNKS)
            def _(c):
                result[s, :, chunk(c)] = stiffness(s, c) - contract(
                    stack[s, K_END, own_terms, :], stack[s, x_at(c), own_terms, :]
                )

        for s in range(OWN):
            arrival(e_recv.at[s], me_recv.at[s], (g, mid))

            @pl.loop(0, CHUNKS)
            def _(c):
                result[s, :, chunk(c)] = result[s, :, chunk(c)] - e_recv[s, c]

        departed(got.at[:, pl.ds(0, FED)], em_send)

    def arrived(s, q):
        if s == 0:
            arrival(from_end.at[0, q], em_recv.at[q], (g, end))
        else:
            for i, (first, count) in enumerate(LATER_FEEDS):
                if first == q:
                    arrival(from_end.at[1, pl.ds(first, count)], em_recv.at[FED + i], (g, end))

    def produce(s, beside=None):
        for q in range(FED):
            arrived(s, q)
            stack_piece(s, q, from_end, 3 * depth)
            kind, c = PIECES[q]
            if kind == X:
                p_send[s, 0, c] = contract(stack[s, K_FAR_END], stack[s, q])
                cross_far_end(s, c).start()
            if beside is not None:
                beside(q)

        def far_mid(first, count):
            @pl.loop(first, first + count)
            def _(c):
                p_send[s, 1, c] = contract(stack[s, K_FAR_MID], stack[s, x_at(c)])

        if s == 0:
            far_mid(0, CHUNKS)
            cross_far_mid(0, 0).start()
        else:
            for i, (first, count) in enumerate(LATER_CROSSES):
                far_mid(first, count)
                cross_far_mid(1, i).start()

    def forward(s):
        for c in range(CHUNKS):
            part = contract(stack[s, K_END, own_terms, :], stack[s, X_AT[c], own_terms, :])
            if s:
                cross_far_end(1, c).wait_recv()
            elif c % 2 == 0:
                arrival(p_recv.at[0, 0, pl.ds(c, 2)], mm_recv.at[c // 2], (g, across))
            e_send[s, c] = p_recv[s, 0, c] + part
            deliver(s, c).start()

    def own_share(s):
        @pl.loop(0, CHUNKS)
        def _(c):
            result[s, :, chunk(c)] = stiffness(s, c) - contract(stack[s, K_MID], stack[s, x_at(c)])

    def finish(s):
        def subtract(first, count):
            @pl.loop(first, first + count)
            def _(c):
                result[s, :, chunk(c)] = result[s, :, chunk(c)] - p_recv[s, 1, c]

        if s == 0:
            cross_far_mid(0, 0).wait_recv()
            subtract(0, CHUNKS)
        else:
            for i, (first, count) in enumerate(LATER_CROSSES):
                cross_far_mid(1, i).wait_recv()
                subtract(first, count)

    def far_arrived(q):
        if q == 2:
            arrival(from_far.at[1, pl.ds(0, 4)], far_recv.at[1], (g, across))
            for p in range(4):
                stack_far(1, p)
        elif q == 4:
            arrival(from_far.at[1, pl.ds(4, 2)], far_recv.at[2], (g, across))
            for p in range(4, FAR):
                stack_far(1, p)
        for c in ((), (), (0, 1), (), (2, 3), (), ())[q]:
            e_send[0, c] = contract(stack[0, K_END, own_terms, :], stack[0, X_AT[c], own_terms, :]) + contract(
                far_stack[K_FAR_END], far_stack[X_AT[c]]
            )
            deliver(0, c).start()

    @pl.when(even_mid)
    def _():
        for q in range(FED):
            arrived(0, q)
            if q < FAR:
                far_end_share(q).start()
            stack_piece(0, q, from_end, 3 * depth)
        arrival(from_far.at[0], far_recv.at[0], (g, across))
        for q in range(FAR):
            stack_far(0, q)
        migrate_b().wait_recv()
        own_share(0)
        produce(1, far_arrived)
        own_share(1)

        @pl.loop(0, CHUNKS)
        def _(c):
            result[0, :, chunk(c)] = result[0, :, chunk(c)] - contract(far_stack[K_FAR_MID], far_stack[x_at(c)])

        forward(1)
        finish(1)
        departed(from_far, far_send)

    @pl.when(odd_mid)
    def _():
        produce(0)
        migrate_b().wait_recv()
        own_share(0)
        forward(0)
        produce(1)
        own_share(1)
        finish(0)
        forward(1)
        finish(1)
        departed(p_send.at[0], mm_send.at[0])

    @pl.when(is_mid)
    def _():
        departed(p_send.at[1], mm_send.at[1])
        departed(e_send, me_send)

    departed(leaving, mig_send.at[0])
    departed(b_out, mig_send.at[1])


def line_body(coupling, interior_solve, boundary_stiffness, migration):
    home, depth, columns = interior_solve.shape
    rows = boundary_stiffness.shape[1]
    width = columns // CHUNKS
    f32, bf16 = jnp.float32, jnp.bfloat16
    b_share, share = (OWN, rows, columns), (OWN, len(PIECES), depth, width)
    pieces = (OWN, CHUNKS, rows, width)
    dma = pltpu.SemaphoreType.DMA
    return pl.pallas_call(
        line_kernel,
        out_shape=pltpu.VMEM(b_share, f32),
        in_specs=[pl.BlockSpec(memory_space=pl.ANY)] * 4,
        out_specs=pl.BlockSpec(memory_space=pltpu.VMEM),
        scratch_shapes=[
            pltpu.SMEM(migration.shape, jnp.int32),
            *[pltpu.VMEM((home, depth // n, width), f32) for _, _, n in UNITS],
            pltpu.VMEM((home, rows, columns), f32),
            pltpu.VMEM(share, f32),
            pltpu.VMEM(b_share, f32),
            pltpu.VMEM(share, f32),
            pltpu.VMEM(b_share, f32),
            pltpu.VMEM(share, f32),
            pltpu.VMEM((OWN, FED, depth, width), f32),
            pltpu.VMEM((2, FAR, depth, width), f32),
            pltpu.VMEM((OWN, len(PIECES), 6 * depth, width), bf16),
            pltpu.VMEM((FAR, 6 * depth, width), bf16),
            pltpu.VMEM((OWN, 2, CHUNKS, rows, width), f32),
            pltpu.VMEM((OWN, 2, CHUNKS, rows, width), f32),
            pltpu.VMEM(pieces, f32),
            pltpu.VMEM(pieces, f32),
            dma((AHEAD + 2,)),
            dma((2,)),
            dma((len(UNITS) + 2,)),
            dma,
            dma((FED + len(LATER_FEEDS),)),
            dma,
            dma((3,)),
            dma((OWN,)),
            dma((3 + CHUNKS + len(LATER_CROSSES),)),
            dma,
            dma((OWN,)),
        ],
        compiler_params=pltpu.CompilerParams(
            collective_id=0, has_side_effects=True, vmem_limit_bytes=60 * 1024 * 1024
        ),
    )(migration, jnp.swapaxes(coupling, 1, 2), interior_solve, boundary_stiffness)


def solution(mesh):
    return jax.shard_map(
        line_body if mesh.shape["tile"] == LINE else portable_body,
        mesh=mesh,
        in_specs=(
            P("group", None, "tile"),
            P("group", "tile", None),
            P("group", "tile", None),
            P(),
        ),
        out_specs=P("group", "tile", None),
        check_vma=False,
    )
```

time: 108 us -> 99.5 us (0.921)
  the two profiles are of different devices: /device:TPU:0 before, /device:TPU:9 now
where the time goes in v2:
time: 99.5 us; the launch traced here: 98.6 us
  Pallas kernels  97.3 us (98%)
  local copies, waits for them, and re-layouts  1.32 us (1%)
    pallas_call x1, Pallas kernels, line_body(): pl.pallas_call(line_kernel, out_shape=pltpu.VMEM(b_share, f32), in_specs=...  97.3 us

profile of v2, /device:TPU:9, one launch (start us, length us, event | category | flops | bytes accessed | tf_op | source)
XLA Modules:
  0.0 98.6 jit_solution(16181322221378771587)
XLA Ops:
  0.0 97.3 %shard_map.46 = f32[2,256,1024]{2,1,0:T(8,128)S(1)} custom-call(s32[32]{0:T(128)} %plan_hbm.1, f32[4,192,1024]{2,1,0:T(8,128)} %bitcast.1, f32[4,192,1024]{2,1,0:T(8,128)} %x_hbm.1, f32[4,256,1024]{2,1,0:T(8,128)} %b_hbm.1), custom_call_target="tpu_custom_call" | custom-call | tf_op jit(solution)/shard_map/pallas_call | solution.py:464
  97.3 1.3 %copy.6 = f32[2,256,1024]{2,1,0:T(8,128)} copy(f32[2,256,1024]{2,1,0:T(8,128)S(1)} %shard_map.46) | data formatting | bytes 4194304

commit v3 on v2

v3 whole, which is shorter than its diff:
```python
import jax
import jax.numpy as jnp
from jax import lax
from jax.experimental import pallas as pl
from jax.experimental.pallas import tpu as pltpu
from jax.sharding import PartitionSpec as P

OWN = 2


def swapped(array, axis, distance):
    return lax.ppermute(array, axis, [(i, i ^ 1 << distance) for i in range(lax.axis_size(axis))])


def condense(coupling_cols, solve_rows, stiff_rows):
    product = lax.psum_scatter(
        jnp.dot(
            coupling_cols,
            solve_rows,
            precision=lax.Precision.HIGHEST,
            preferred_element_type=jnp.float32,
        ),
        "tile",
        scatter_dimension=0,
        tiled=True,
    )
    return stiff_rows - product


def select_slots(stacked, positions, present):
    chosen = jnp.take(stacked, positions, axis=0)
    shaped = present.reshape((-1,) + (1,) * (stacked.ndim - 1))
    return jnp.where(shaped, chosen, jnp.zeros_like(chosen))


def portable_body(coupling, interior_solve, boundary_stiffness, migration):
    home_count = coupling.shape[0]
    mygroup = lax.axis_index("group")
    partner = jnp.bitwise_xor(mygroup, 1)
    own_plan = lax.dynamic_slice_in_dim(migration, mygroup * home_count, home_count)
    slot_ids = jnp.arange(OWN, dtype=jnp.int32)
    local_ids = jnp.arange(home_count, dtype=jnp.int32)

    def locate(wanted):
        matches = own_plan[None, :] == wanted[:, None]
        positions = jnp.sum(jnp.where(matches, local_ids[None, :], 0), axis=1)
        return (positions, jnp.any(matches, axis=1))

    mine_index, mine_here = locate(mygroup * OWN + slot_ids)
    their_index, their_here = locate(partner * OWN + slot_ids)
    keep_mask = mine_here[:, None, None]
    outgoing = (
        select_slots(coupling, their_index, their_here),
        select_slots(interior_solve, their_index, their_here),
        select_slots(boundary_stiffness, their_index, their_here),
    )
    arrived = swapped((outgoing[0], outgoing[1], outgoing[2]), "group", 0)
    kept_coupling = jnp.where(keep_mask, jnp.take(coupling, mine_index, axis=0), arrived[0])
    kept_solve = jnp.where(keep_mask, jnp.take(interior_solve, mine_index, axis=0), arrived[1])
    kept_stiff = jnp.where(keep_mask, jnp.take(boundary_stiffness, mine_index, axis=0), arrived[2])
    result = jnp.stack(
        [condense(kept_coupling[slot], kept_solve[slot], kept_stiff[slot]) for slot in range(OWN)]
    )
    return result


MESH = pl.DeviceIdType.MESH
LINE = 4
CHUNKS = 4
STRIP = 64
AHEAD = 4
LAG = 2
K, X = 0, 1
PIECES = ((K, 0), (X, 0), (K, 1), (X, 1), (X, 2), (X, 3), (K, 2), (K, 3))
K_FAR_END, K_FAR_MID, K_MID, K_END = 0, 2, 6, 7
X_AT = (1, 3, 4, 5)
UNITS = ((0, 0, 1), (0, 1, 2), (0, 3, 3)) + tuple((q, 0, 6) for q in range(1, len(PIECES)))
GROUPS = ((0,), (1,), (2,), (3,), (4,), (5, 6, 7), (8, 9))
FED = 7
FAR = 6
LATER_FEEDS = ((0, 2), (2, 2), (4, 2), (6, 1))
CROSSES = (((0, 1), (1, 3)), ((0, 1), (1, 2), (3, 1)))


def split_into(stack, base, depth, rows, value, order):
    high = value.astype(jnp.bfloat16)
    low = (value - high.astype(jnp.float32)).astype(jnp.bfloat16)
    for place, term in enumerate(order):
        stack[pl.ds(base + place * depth + rows, value.shape[0]), :] = high if term == 0 else low


def contract(left, right):
    return lax.dot_general(left, right, (((0,), (0,)), ((), ())), preferred_element_type=jnp.float32)


def strips(count, body):
    strip = STRIP if count % STRIP == 0 else STRIP // 2

    @pl.loop(0, count // strip)
    def _(i):
        first = pl.multiple_of(i * strip, strip)
        body(first, pl.ds(first, strip))


def line_kernel(plan_hbm, k_hbm, x_hbm, b_hbm, result, plan, *scratch):
    homes, scratch = scratch[: len(UNITS)], scratch[len(UNITS) :]
    (
        b_home, leaving, b_out, coming, b_in, got, from_end, from_far, stack, far_stack,
        p_send, p_recv, e_send, e_recv,
        mm_send, mm_recv, me_send, me_recv,
    ) = scratch
    home, _, width = homes[0].shape
    depth = got.shape[2]
    rows = b_home.shape[1]
    last = LINE - 1
    g, t = lax.axis_index("group"), lax.axis_index("tile")
    parity = g % 2
    partner = g + 1 - 2 * parity
    side = t // 2
    end, mid = side * last, 1 + side
    far_end, across = last - end, last - mid
    is_end = t == end
    is_mid = t == mid
    even_mid = is_mid & (parity == 0)
    odd_mid = is_mid & (parity == 1)

    def chunk(index):
        return pl.ds(pl.multiple_of(index * width, width), width)

    def remote(src, dst, send_sem, recv_sem, to):
        return pltpu.make_async_remote_copy(
            src_ref=src, dst_ref=dst, send_sem=send_sem, recv_sem=recv_sem, device_id=to, device_id_type=MESH
        )

    def cross_far_end(s, first, count):
        at = pl.ds(first, count)
        return remote(
            p_send.at[s, 0, at], p_recv.at[s, 0, at], mm_send.at[s], mm_recv.at[2 * s + first // 2], (g, across)
        )

    def cross_far_mid(s, i):
        at = pl.ds(*CROSSES[s][i])
        return remote(
            p_send.at[s, 1, at], p_recv.at[s, 1, at], mm_send.at[s], mm_recv.at[2 * OWN + (1 + i if s else 0)], (g, across)
        )

    def deliver(s, half):
        at = pl.ds(2 * half, 2)
        return remote(e_send.at[s, at], e_recv.at[s, at], me_send, me_recv, (g, end))

    def arrival(buffer, sem, source):
        remote(buffer, buffer, sem, sem, source).wait_recv()

    def departed(buffer, sem):
        remote(buffer, buffer, sem, sem, (partner, t)).wait_send()

    own_terms = pl.ds(0, 3 * depth)

    def x_at(c):
        return jnp.where(c == 0, X_AT[0], c + X_AT[1] - 1)

    def forward(s):
        for half in range(2):
            at = pl.ds(2 * half, 2)
            for c in (2 * half, 2 * half + 1):
                e_send[s, c] = contract(stack[s, K_END, own_terms, :], stack[s, X_AT[c], own_terms, :])
            arrival(p_recv.at[s, 0, at], mm_recv.at[2 * s + half], (g, across))
            for c in (2 * half, 2 * half + 1):
                e_send[s, c] = e_send[s, c] + p_recv[s, 0, c]
            deliver(s, half).start()

    def finish(s):
        def subtract(first, count):
            @pl.loop(first, first + count)
            def _(c):
                result[s, :, chunk(c)] = result[s, :, chunk(c)] - p_recv[s, 1, c]

        if s == 0:
            arrival(p_recv.at[0, 1], mm_recv.at[2 * OWN], (g, across))
            subtract(0, CHUNKS)
        else:
            for i, (first, count) in enumerate(CROSSES[1]):
                cross_far_mid(1, i).wait_recv()
                subtract(first, count)

    def first_phase(load_sem, mig_send, mig_recv, em_send, em_recv, far_send, far_recv):
        def part(u):
            q, first, count = UNITS[u]
            return q, first * (depth // 6), count * (depth // 6)

        def span(group):
            units = [part(u) for u in group]
            if len(group) == 1:
                q, first, count = units[0]
                return q, pl.ds(first, count)
            return pl.ds(units[0][0], len(group)), pl.ds(0, depth)

        def load(u, which=slice(None)):
            q, first, count = part(u)
            kind, n = PIECES[q]
            at = chunk(n if kind == X else (far_end, across, mid, end)[n])
            return pltpu.make_async_copy(
                (k_hbm, x_hbm)[kind].at[which, pl.ds(first, count), at], homes[u].at[which], load_sem.at[u % AHEAD]
            )

        b_load = pltpu.make_async_copy(b_hbm, b_home, load_sem.at[AHEAD])
        plan_load = pltpu.make_async_copy(plan_hbm, plan, load_sem.at[AHEAD + 1])
        plan_load.start()
        for j in range(home):
            load(0, pl.ds(j, 1)).start()
        for u in range(1, AHEAD):
            load(u).start()

        barrier = pltpu.get_barrier_semaphore()
        pl.semaphore_signal(barrier, inc=1, device_id=(partner, t), device_id_type=MESH)

        @pl.when(is_mid)
        def _():
            pl.semaphore_signal(barrier, inc=1, device_id=(g, across), device_id_type=MESH)
            pl.semaphore_signal(barrier, inc=1, device_id=(g, end), device_id_type=MESH)

        plan_load.wait()

        def find(wanted):
            index, here = jnp.int32(0), jnp.int32(0)
            for j in range(home):
                hit = plan[g * home + j] == wanted
                index, here = jnp.where(hit, j, index), jnp.where(hit, 1, here)
            return index, here > 0

        mine = [find(g * OWN + s) for s in range(OWN)]
        theirs = [find(partner * OWN + s) for s in range(OWN)]

        def migrate(i):
            q, at = span(GROUPS[i])
            return remote(leaving.at[0, q, at], coming.at[0, q, at], mig_send.at[0], mig_recv.at[i], (partner, t))

        def migrate_later():
            return remote(leaving.at[1], coming.at[1], mig_send.at[0], mig_recv.at[len(GROUPS)], (partner, t))

        def migrate_b():
            return remote(b_out, b_in, mig_send.at[1], mig_recv.at[len(GROUPS) + 1], (partner, t))

        def feed(q, to):
            return remote(got.at[0, q], from_end.at[0, q], em_send, em_recv.at[q], (g, to))

        def feed_later(i, to):
            at = pl.ds(*LATER_FEEDS[i])
            return remote(got.at[1, at], from_end.at[1, at], em_send, em_recv.at[FED + i], (g, to))

        def far_own(i):
            q, at = span(GROUPS[i])
            return remote(got.at[0, q, at], from_far.at[0, q, at], far_send, far_recv.at[0], (g, across))

        def far_end_share(q):
            return remote(from_end.at[0, q], from_far.at[1, q], far_send, far_recv.at[1 + q // 4], (g, across))

        def gather(u, s):
            q, first, count = part(u)

            def copy(at, rows_at):
                leaving[s, q, pl.ds(first + at, rows_at.size), :] = homes[u][theirs[s][0], rows_at, :]

            strips(count, copy)

        def settle(u, s):
            q, first, count = part(u)
            index, here = mine[s]

            def choose(at, rows_at):
                place = pl.ds(first + at, rows_at.size)
                got[s, q, place, :] = jnp.where(here, homes[u][index, rows_at, :], coming[s, q, place, :])

            strips(count, choose)

        def settle_first(i):
            migrate(i).wait_recv()
            for u in GROUPS[i]:
                q, first, count = part(u)
                settle(u, 0)
                if q < FED and first + count == depth:
                    @pl.when(is_end)
                    def _():
                        feed(q, mid).start()

            if part(GROUPS[i][0])[0] < FAR:
                @pl.when(even_mid)
                def _():
                    far_own(i).start()

        for i, group in enumerate(GROUPS):
            for u in group:
                load(u).wait()
                if u + AHEAD < len(UNITS):
                    load(u + AHEAD).start()
                elif u + AHEAD == len(UNITS):
                    b_load.start()
                gather(u, 0)
            if i == 0:
                pl.semaphore_wait(barrier, 2)
            migrate(i).start()
            if i >= LAG:
                settle_first(i - LAG)
            for u in group:
                gather(u, 1)
        migrate_later().start()
        for i in range(len(GROUPS) - LAG, len(GROUPS)):
            settle_first(i)

        def stack_piece(s, q, source, base):
            order = ((0, 0, 1), (0, 1, 0))[PIECES[q][0]]
            strips(depth, lambda first, at: split_into(stack.at[s, q], base, depth, first, source[s, q, at, :], order))

        def stack_far(source, q):
            order = ((0, 0, 1), (0, 1, 0))[PIECES[q][0]]
            strips(depth, lambda first, at: split_into(
                far_stack.at[q], 3 * source * depth, depth, first, from_far[source, q, at, :], order
            ))

        own_pieces = (K_END,) + X_AT

        @pl.when(is_mid)
        def _():
            for q in range(len(PIECES)):
                stack_piece(0, q, got, 0)

        migrate_later().wait_recv()
        for u in range(len(UNITS)):
            settle(u, 1)

        @pl.when(is_end)
        def _():
            for i in range(len(LATER_FEEDS)):
                feed_later(i, mid).start()

        @pl.when(is_mid)
        def _():
            for q in range(len(PIECES)):
                stack_piece(1, q, got, 0)

        b_load.wait()
        for s in range(OWN):
            def copy(_, at):
                b_out[s, at, :] = b_home[theirs[s][0], at, :]

            strips(rows, copy)
        migrate_b().start()

        def stiffness(s, c):
            index, here = mine[s]
            return jnp.where(here, b_home[index, :, chunk(c)], b_in[s, :, chunk(c)])

        @pl.when(is_end)
        def _():
            for s in range(OWN):
                for q in own_pieces:
                    stack_piece(s, q, got, 0)
            migrate_b().wait_recv()
            for s in range(OWN):
                @pl.loop(0, CHUNKS)
                def _(c):
                    result[s, :, chunk(c)] = stiffness(s, c) - contract(
                        stack[s, K_END, own_terms, :], stack[s, x_at(c), own_terms, :]
                    )

            departed(got.at[:, pl.ds(0, FED)], em_send)

        def arrived(s, q):
            if s == 0:
                arrival(from_end.at[0, q], em_recv.at[q], (g, end))
            else:
                for i, (first, count) in enumerate(LATER_FEEDS):
                    if first == q:
                        arrival(from_end.at[1, pl.ds(first, count)], em_recv.at[FED + i], (g, end))

        def produce(s, beside=None):
            early = beside is None

            def far_mid(i):
                first, count = CROSSES[s][i]

                @pl.loop(first, first + count)
                def _(c):
                    p_send[s, 1, c] = contract(stack[s, K_FAR_MID], stack[s, x_at(c)])

                cross_far_mid(s, i).start()

            for q in range(FED):
                arrived(s, q)
                stack_piece(s, q, from_end, 3 * depth)
                kind, c = PIECES[q]
                if kind == X:
                    p_send[s, 0, c] = contract(stack[s, K_FAR_END], stack[s, q])
                    if s == 0 or c < 2:
                        cross_far_end(s, c, 1).start()
                    elif c == 3:
                        cross_far_end(s, 2, 2).start()
                if early and q == (3 if s else 2):
                    far_mid(0)
                if beside is not None:
                    beside(q)
            for i in range(int(early), len(CROSSES[s])):
                far_mid(i)

        def own_share(s):
            @pl.loop(0, CHUNKS)
            def _(c):
                result[s, :, chunk(c)] = stiffness(s, c) - contract(stack[s, K_MID], stack[s, x_at(c)])

        def far_arrived(q):
            if q == 2:
                arrival(from_far.at[1, pl.ds(0, 4)], far_recv.at[1], (g, across))
                for p in range(4):
                    stack_far(1, p)
            elif q == 4:
                arrival(from_far.at[1, pl.ds(4, 2)], far_recv.at[2], (g, across))
                for p in range(4, FAR):
                    stack_far(1, p)
            for c in ((), (), (0, 1), (), (2, 3), (), ())[q]:
                e_send[0, c] = contract(stack[0, K_END, own_terms, :], stack[0, X_AT[c], own_terms, :]) + contract(
                    far_stack[K_FAR_END], far_stack[X_AT[c]]
                )
                if c % 2:
                    deliver(0, c // 2).start()

        @pl.when(even_mid)
        def _():
            for q in range(FED):
                arrived(0, q)
                if q < FAR:
                    far_end_share(q).start()
                stack_piece(0, q, from_end, 3 * depth)
            arrival(from_far.at[0], far_recv.at[0], (g, across))
            for q in range(FAR):
                stack_far(0, q)
            migrate_b().wait_recv()
            own_share(0)
            produce(1, far_arrived)
            own_share(1)

            @pl.loop(0, CHUNKS)
            def _(c):
                result[0, :, chunk(c)] = result[0, :, chunk(c)] - contract(far_stack[K_FAR_MID], far_stack[x_at(c)])

            departed(from_far, far_send)

        @pl.when(odd_mid)
        def _():
            produce(0)
            migrate_b().wait_recv()
            own_share(0)
            forward(0)
            produce(1)
            own_share(1)
            finish(0)
            departed(p_send.at[0], mm_send.at[0])

        departed(leaving, mig_send.at[0])
        departed(b_out, mig_send.at[1])
    dma = pltpu.SemaphoreType.DMA
    pl.run_scoped(
        first_phase, dma((AHEAD + 2,)), dma((2,)), dma((len(GROUPS) + 2,)), dma, dma((FED + len(LATER_FEEDS),)), dma, dma((3,))
    )

    @pl.when(is_end)
    def _():
        arrival(e_recv, me_recv, (g, mid))
        for s in range(OWN):
            @pl.loop(0, CHUNKS)
            def _(c):
                result[s, :, chunk(c)] = result[s, :, chunk(c)] - e_recv[s, c]


    @pl.when(is_mid)
    def _():
        forward(1)
        finish(1)
        departed(p_send.at[1], mm_send.at[1])
        departed(e_send, me_send)


def line_body(coupling, interior_solve, boundary_stiffness, migration):
    home, depth, columns = interior_solve.shape
    rows = boundary_stiffness.shape[1]
    width = columns // CHUNKS
    f32, bf16 = jnp.float32, jnp.bfloat16
    b_share, share = (OWN, rows, columns), (OWN, len(PIECES), depth, width)
    pieces = (OWN, CHUNKS, rows, width)
    dma = pltpu.SemaphoreType.DMA
    return pl.pallas_call(
        line_kernel,
        out_shape=pltpu.VMEM(b_share, f32),
        in_specs=[pl.BlockSpec(memory_space=pl.ANY)] * 4,
        out_specs=pl.BlockSpec(memory_space=pltpu.VMEM),
        scratch_shapes=[
            pltpu.SMEM(migration.shape, jnp.int32),
            *[pltpu.VMEM((home, depth // 6 * n, width), f32) for _, _, n in UNITS],
            pltpu.VMEM((home, rows, columns), f32),
            pltpu.VMEM(share, f32),
            pltpu.VMEM(b_share, f32),
            pltpu.VMEM(share, f32),
            pltpu.VMEM(b_share, f32),
            pltpu.VMEM(share, f32),
            pltpu.VMEM((OWN, FED, depth, width), f32),
            pltpu.VMEM((2, FAR, depth, width), f32),
            pltpu.VMEM((OWN, len(PIECES), 6 * depth, width), bf16),
            pltpu.VMEM((FAR, 6 * depth, width), bf16),
            pltpu.VMEM((OWN, 2, CHUNKS, rows, width), f32),
            pltpu.VMEM((OWN, 2, CHUNKS, rows, width), f32),
            pltpu.VMEM(pieces, f32),
            pltpu.VMEM(pieces, f32),
            dma((OWN,)),
            dma((2 * OWN + 1 + len(CROSSES[1]),)),
            dma,
            dma,
        ],
        compiler_params=pltpu.CompilerParams(
            collective_id=0, has_side_effects=True, vmem_limit_bytes=60 * 1024 * 1024
        ),
    )(migration, jnp.swapaxes(coupling, 1, 2), interior_solve, boundary_stiffness)


def solution(mesh):
    return jax.shard_map(
        line_body if mesh.shape["tile"] == LINE else portable_body,
        mesh=mesh,
        in_specs=(
            P("group", None, "tile"),
            P("group", "tile", None),
            P("group", "tile", None),
            P(),
        ),
        out_specs=P("group", "tile", None),
        check_vma=False,
    )
```

time: 99.5 us -> 98.8 us (level)
  Pallas kernels: 97.3 us -> 96 us
    pallas_call x1, Pallas kernels: 97.3 us -> 96 us  [line_body(): pl.pallas_call(line_kernel, out_shape=pltpu.VMEM(b_share, f32), in_specs=...]
where the time goes in v3:
time: 98.8 us; the launch traced here: 97.3 us
  Pallas kernels  96 us (97%)
  local copies, waits for them, and re-layouts  1.32 us (1%)
    pallas_call x1, Pallas kernels, line_body(): pl.pallas_call(line_kernel, out_shape=pltpu.VMEM(b_share, f32), in_specs=...  96 us

profile of v3, /device:TPU:9, one launch (start us, length us, event | category | flops | bytes accessed | tf_op | source)
XLA Modules:
  0.0 97.3 jit_solution(3119931717850286745)
XLA Ops:
  0.0 96.0 %shard_map.46 = f32[2,256,1024]{2,1,0:T(8,128)S(1)} custom-call(s32[32]{0:T(128)} %plan_hbm.1, f32[4,192,1024]{2,1,0:T(8,128)} %bitcast.1, f32[4,192,1024]{2,1,0:T(8,128)} %x_hbm.1, f32[4,256,1024]{2,1,0:T(8,128)} %b_hbm.1), custom_call_target="tpu_custom_call" | custom-call | tf_op jit(solution)/shard_map/pallas_call | solution.py:490
  96.0 1.3 %copy.6 = f32[2,256,1024]{2,1,0:T(8,128)} copy(f32[2,256,1024]{2,1,0:T(8,128)S(1)} %shard_map.46) | data formatting | bytes 4194304

commit v4 on v3

--- a/solution.py
+++ b/solution.py
@@ -135,13 +135,13 @@
     def cross_far_end(s, first, count):
         at = pl.ds(first, count)
         return remote(
-            p_send.at[s, 0, at], p_recv.at[s, 0, at], mm_send.at[s], mm_recv.at[2 * s + first // 2], (g, across)
+            p_send.at[s, 0, at], p_recv.at[s, 0, at], crossing[s][0], crossing[s][1].at[first // 2], (g, across)
         )
 
     def cross_far_mid(s, i):
         at = pl.ds(*CROSSES[s][i])
         return remote(
-            p_send.at[s, 1, at], p_recv.at[s, 1, at], mm_send.at[s], mm_recv.at[2 * OWN + (1 + i if s else 0)], (g, across)
+            p_send.at[s, 1, at], p_recv.at[s, 1, at], crossing[s][0], crossing[s][1].at[2 + (i if s else 0)], (g, across)
         )
 
     def deliver(s, half):
@@ -164,7 +164,7 @@
             at = pl.ds(2 * half, 2)
             for c in (2 * half, 2 * half + 1):
                 e_send[s, c] = contract(stack[s, K_END, own_terms, :], stack[s, X_AT[c], own_terms, :])
-            arrival(p_recv.at[s, 0, at], mm_recv.at[2 * s + half], (g, across))
+            arrival(p_recv.at[s, 0, at], crossing[s][1].at[half], (g, across))
             for c in (2 * half, 2 * half + 1):
                 e_send[s, c] = e_send[s, c] + p_recv[s, 0, c]
             deliver(s, half).start()
@@ -176,14 +176,20 @@
                 result[s, :, chunk(c)] = result[s, :, chunk(c)] - p_recv[s, 1, c]
 
         if s == 0:
-            arrival(p_recv.at[0, 1], mm_recv.at[2 * OWN], (g, across))
+            arrival(p_recv.at[0, 1], crossing[0][1].at[2], (g, across))
             subtract(0, CHUNKS)
         else:
             for i, (first, count) in enumerate(CROSSES[1]):
                 cross_far_mid(1, i).wait_recv()
                 subtract(first, count)
 
-    def first_phase(load_sem, mig_send, mig_recv, em_send, em_recv, far_send, far_recv):
+    crossing = {1: (mm_send, mm_recv)}
+
+    def first_phase(
+        load_sem, mig_send, mig_recv, em_send, em_recv, far_send, far_recv, first_send, first_recv
+    ):
+        crossing[0] = (first_send, first_recv)
+
         def part(u):
             q, first, count = UNITS[u]
             return q, first * (depth // 6), count * (depth // 6)
@@ -374,8 +380,6 @@
                         arrival(from_end.at[1, pl.ds(first, count)], em_recv.at[FED + i], (g, end))
 
         def produce(s, beside=None):
-            early = beside is None
-
             def far_mid(i):
                 first, count = CROSSES[s][i]
 
@@ -395,11 +399,11 @@
                         cross_far_end(s, c, 1).start()
                     elif c == 3:
                         cross_far_end(s, 2, 2).start()
-                if early and q == (3 if s else 2):
+                if q == (3 if s else 2):
                     far_mid(0)
                 if beside is not None:
                     beside(q)
-            for i in range(int(early), len(CROSSES[s])):
+            for i in range(1, len(CROSSES[s])):
                 far_mid(i)
 
         def own_share(s):
@@ -453,13 +457,14 @@
             produce(1)
             own_share(1)
             finish(0)
-            departed(p_send.at[0], mm_send.at[0])
+            departed(p_send.at[0], first_send)
 
         departed(leaving, mig_send.at[0])
         departed(b_out, mig_send.at[1])
     dma = pltpu.SemaphoreType.DMA
     pl.run_scoped(
-        first_phase, dma((AHEAD + 2,)), dma((2,)), dma((len(GROUPS) + 2,)), dma, dma((FED + len(LATER_FEEDS),)), dma, dma((3,))
+        first_phase, dma((AHEAD + 2,)), dma((2,)), dma((len(GROUPS) + 2,)), dma, dma((FED + len(LATER_FEEDS),)),
+        dma, dma((3,)), dma, dma((3,)),
     )
 
     @pl.when(is_end)
@@ -475,7 +480,7 @@
     def _():
         forward(1)
         finish(1)
-        departed(p_send.at[1], mm_send.at[1])
+        departed(p_send.at[1], mm_send)
         departed(e_send, me_send)
 
 
@@ -509,8 +514,8 @@
             pltpu.VMEM((OWN, 2, CHUNKS, rows, width), f32),
             pltpu.VMEM(pieces, f32),
             pltpu.VMEM(pieces, f32),
-            dma((OWN,)),
-            dma((2 * OWN + 1 + len(CROSSES[1]),)),
+            dma,
+            dma((2 + len(CROSSES[1]),)),
             dma,
             dma,
         ],

time: 98.8 us -> 98.7 us (level); the launches traced: 97.3 us -> 98.6 us
  Pallas kernels: 96 us -> 97.2 us
    pallas_call x1, Pallas kernels: 96 us -> 97.2 us  [line_body(): pl.pallas_call(line_kernel, out_shape=pltpu.VMEM(b_share, f32), in_specs=...]
where the time goes in v4:
time: 98.7 us; the launch traced here: 98.6 us
  Pallas kernels  97.2 us (98%)
  local copies, waits for them, and re-layouts  1.32 us (1%)
    pallas_call x1, Pallas kernels, line_body(): pl.pallas_call(line_kernel, out_shape=pltpu.VMEM(b_share, f32), in_specs=...  97.2 us

profile of v4, /device:TPU:9, one launch (start us, length us, event | category | flops | bytes accessed | tf_op | source)
XLA Modules:
  0.0 98.6 jit_solution(7556477550608126318)
XLA Ops:
  0.0 97.2 %shard_map.46 = f32[2,256,1024]{2,1,0:T(8,128)S(1)} custom-call(s32[32]{0:T(128)} %plan_hbm.1, f32[4,192,1024]{2,1,0:T(8,128)} %bitcast.1, f32[4,192,1024]{2,1,0:T(8,128)} %x_hbm.1, f32[4,256,1024]{2,1,0:T(8,128)} %b_hbm.1), custom_call_target="tpu_custom_call" | custom-call | tf_op jit(solution)/shard_map/pallas_call | solution.py:495
  97.3 1.3 %copy.6 = f32[2,256,1024]{2,1,0:T(8,128)} copy(f32[2,256,1024]{2,1,0:T(8,128)S(1)} %shard_map.46) | data formatting | bytes 4194304

commit v5 on v3

--- a/solution.py
+++ b/solution.py
@@ -68,14 +68,16 @@
 LINE = 4
 CHUNKS = 4
 STRIP = 64
-AHEAD = 4
+AHEAD = 5
 LAG = 2
 K, X = 0, 1
 PIECES = ((K, 0), (X, 0), (K, 1), (X, 1), (X, 2), (X, 3), (K, 2), (K, 3))
 K_FAR_END, K_FAR_MID, K_MID, K_END = 0, 2, 6, 7
 X_AT = (1, 3, 4, 5)
-UNITS = ((0, 0, 1), (0, 1, 2), (0, 3, 3)) + tuple((q, 0, 6) for q in range(1, len(PIECES)))
-GROUPS = ((0,), (1,), (2,), (3,), (4,), (5, 6, 7), (8, 9))
+UNITS = ((0, 0, 1), (0, 1, 1), (0, 2, 2), (0, 4, 2)) + tuple((q, 0, 6) for q in range(1, len(PIECES)))
+GROUPS = ((0,), (1,), (2,), (3,), (4,), (5,), (6, 7, 8), (9, 10))
+TWICE = 1
+FAR_SEMS = (0, 0, 1, 1, 2, 2, 2)
 FED = 7
 FAR = 6
 LATER_FEEDS = ((0, 2), (2, 2), (4, 2), (6, 1))
@@ -105,7 +107,7 @@
 def line_kernel(plan_hbm, k_hbm, x_hbm, b_hbm, result, plan, *scratch):
     homes, scratch = scratch[: len(UNITS)], scratch[len(UNITS) :]
     (
-        b_home, leaving, b_out, coming, b_in, got, from_end, from_far, stack, far_stack,
+        b_home, leaving, b_out, coming, b_in, got, from_end, from_far, own_try, far_tries, stack, far_stack,
         p_send, p_recv, e_send, e_recv,
         mm_send, mm_recv, me_send, me_recv,
     ) = scratch
@@ -121,8 +123,8 @@
     far_end, across = last - end, last - mid
     is_end = t == end
     is_mid = t == mid
-    even_mid = is_mid & (parity == 0)
-    odd_mid = is_mid & (parity == 1)
+    factor_mid = is_mid & (parity == 1)
+    other_mid = is_mid & (parity == 0)
 
     def chunk(index):
         return pl.ds(pl.multiple_of(index * width, width), width)
@@ -183,7 +185,7 @@
                 cross_far_mid(1, i).wait_recv()
                 subtract(first, count)
 
-    def first_phase(load_sem, mig_send, mig_recv, em_send, em_recv, far_send, far_recv):
+    def first_phase(load_sem, mig_send, mig_recv, em_send, em_recv, far_send, far_recv, try_send, try_recv):
         def part(u):
             q, first, count = UNITS[u]
             return q, first * (depth // 6), count * (depth // 6)
@@ -219,6 +221,10 @@
             pl.semaphore_signal(barrier, inc=1, device_id=(g, across), device_id_type=MESH)
             pl.semaphore_signal(barrier, inc=1, device_id=(g, end), device_id_type=MESH)
 
+        @pl.when(factor_mid)
+        def _():
+            pl.semaphore_signal(barrier, inc=1, device_id=(partner, across), device_id_type=MESH)
+
         plan_load.wait()
 
         def find(wanted):
@@ -250,10 +256,10 @@
 
         def far_own(i):
             q, at = span(GROUPS[i])
-            return remote(got.at[0, q, at], from_far.at[0, q, at], far_send, far_recv.at[0], (g, across))
+            return remote(got.at[0, q, at], from_far.at[0, q, at], far_send, far_recv.at[FAR_SEMS[i]], (g, across))
 
         def far_end_share(q):
-            return remote(from_end.at[0, q], from_far.at[1, q], far_send, far_recv.at[1 + q // 4], (g, across))
+            return remote(from_end.at[0, q], from_far.at[1, q], far_send, far_recv.at[3 + q // 4], (g, across))
 
         def gather(u, s):
             q, first, count = part(u)
@@ -272,6 +278,22 @@
                 got[s, q, place, :] = jnp.where(here, homes[u][index, rows_at, :], coming[s, q, place, :])
 
             strips(count, choose)
+
+        def send_tries():
+            q, first, count = part(TWICE)
+
+            @pl.when(factor_mid)
+            def _():
+                def copy(_, at):
+                    own_try[at, :] = homes[TWICE][mine[0][0], at, :]
+
+                strips(count, copy)
+                remote(own_try, far_tries.at[0], far_send, try_recv.at[0], (g, across)).start()
+
+            @pl.when(other_mid)
+            def _():
+                mine_of_partner = leaving.at[0, q, pl.ds(first, count)]
+                remote(mine_of_partner, far_tries.at[1], try_send, try_recv.at[1], (partner, across)).start()
 
         def settle_first(i):
             migrate(i).wait_recv()
@@ -283,8 +305,8 @@
                     def _():
                         feed(q, mid).start()
 
-            if part(GROUPS[i][0])[0] < FAR:
-                @pl.when(even_mid)
+            if i != TWICE and part(GROUPS[i][0])[0] < FAR:
+                @pl.when(factor_mid)
                 def _():
                     far_own(i).start()
 
@@ -297,7 +319,16 @@
                     b_load.start()
                 gather(u, 0)
             if i == 0:
-                pl.semaphore_wait(barrier, 2)
+                @pl.when(other_mid)
+                def _():
+                    pl.semaphore_wait(barrier, 3)
+
+                @pl.when(jnp.logical_not(other_mid))
+                def _():
+                    pl.semaphore_wait(barrier, 2)
+
+            if i == TWICE:
+                send_tries()
             migrate(i).start()
             if i >= LAG:
                 settle_first(i - LAG)
@@ -409,11 +440,11 @@
 
         def far_arrived(q):
             if q == 2:
-                arrival(from_far.at[1, pl.ds(0, 4)], far_recv.at[1], (g, across))
+                arrival(from_far.at[1, pl.ds(0, 4)], far_recv.at[3], (g, across))
                 for p in range(4):
                     stack_far(1, p)
             elif q == 4:
-                arrival(from_far.at[1, pl.ds(4, 2)], far_recv.at[2], (g, across))
+                arrival(from_far.at[1, pl.ds(4, 2)], far_recv.at[4], (g, across))
                 for p in range(4, FAR):
                     stack_far(1, p)
             for c in ((), (), (0, 1), (), (2, 3), (), ())[q]:
@@ -423,14 +454,20 @@
                 if c % 2:
                     deliver(0, c // 2).start()
 
-        @pl.when(even_mid)
+        @pl.when(factor_mid)
         def _():
             for q in range(FED):
                 arrived(0, q)
                 if q < FAR:
                     far_end_share(q).start()
                 stack_piece(0, q, from_end, 3 * depth)
-            arrival(from_far.at[0], far_recv.at[0], (g, across))
+            arrival(far_tries.at[0], try_recv.at[0], (g, across))
+            arrival(far_tries.at[1], try_recv.at[1], (partner, across))
+            q, first, count = part(TWICE)
+            from_far[0, q, pl.ds(first, count), :] = jnp.where(mine[0][1], far_tries[0], far_tries[1])
+            arrival(from_far.at[0, 0, pl.ds(0, first)], far_recv.at[0], (g, across))
+            arrival(from_far.at[0, 0, pl.ds(first + count, depth - first - count)], far_recv.at[1], (g, across))
+            arrival(from_far.at[0, pl.ds(1, FAR - 1)], far_recv.at[2], (g, across))
             for q in range(FAR):
                 stack_far(0, q)
             migrate_b().wait_recv()
@@ -444,7 +481,7 @@
 
             departed(from_far, far_send)
 
-        @pl.when(odd_mid)
+        @pl.when(other_mid)
         def _():
             produce(0)
             migrate_b().wait_recv()
@@ -454,12 +491,14 @@
             own_share(1)
             finish(0)
             departed(p_send.at[0], mm_send.at[0])
+            departed(far_tries.at[1], try_send)
 
         departed(leaving, mig_send.at[0])
         departed(b_out, mig_send.at[1])
     dma = pltpu.SemaphoreType.DMA
     pl.run_scoped(
-        first_phase, dma((AHEAD + 2,)), dma((2,)), dma((len(GROUPS) + 2,)), dma, dma((FED + len(LATER_FEEDS),)), dma, dma((3,))
+        first_phase, dma((AHEAD + 2,)), dma((2,)), dma((len(GROUPS) + 2,)), dma, dma((FED + len(LATER_FEEDS),)),
+        dma, dma((5,)), dma, dma((2,)),
     )
 
     @pl.when(is_end)
@@ -503,6 +542,8 @@
             pltpu.VMEM(share, f32),
             pltpu.VMEM((OWN, FED, depth, width), f32),
             pltpu.VMEM((2, FAR, depth, width), f32),
+            pltpu.VMEM((depth // 6, width), f32),
+            pltpu.VMEM((2, depth // 6, width), f32),
             pltpu.VMEM((OWN, len(PIECES), 6 * depth, width), bf16),
             pltpu.VMEM((FAR, 6 * depth, width), bf16),
             pltpu.VMEM((OWN, 2, CHUNKS, rows, width), f32),

time: 98.8 us -> 98.4 us (level); the launches traced: 97.3 us -> 98.3 us
  no operation moved by 1% of the time
where the time goes in v5:
time: 98.4 us; the launch traced here: 98.3 us
  Pallas kernels  96.9 us (98%)
  local copies, waits for them, and re-layouts  1.32 us (1%)
    pallas_call x1, Pallas kernels, line_body(): pl.pallas_call(line_kernel, out_shape=pltpu.VMEM(b_share, f32), in_specs=...  96.9 us

profile of v5, /device:TPU:9, one launch (start us, length us, event | category | flops | bytes accessed | tf_op | source)
XLA Modules:
  0.0 98.3 jit_solution(13047972774310938171)
XLA Ops:
  0.0 96.9 %shard_map.46 = f32[2,256,1024]{2,1,0:T(8,128)S(1)} custom-call(s32[32]{0:T(128)} %plan_hbm.1, f32[4,192,1024]{2,1,0:T(8,128)} %bitcast.1, f32[4,192,1024]{2,1,0:T(8,128)} %x_hbm.1, f32[4,256,1024]{2,1,0:T(8,128)} %b_hbm.1), custom_call_target="tpu_custom_call" | custom-call | tf_op jit(solution)/shard_map/pallas_call | solution.py:529
  96.9 1.3 %copy.6 = f32[2,256,1024]{2,1,0:T(8,128)} copy(f32[2,256,1024]{2,1,0:T(8,128)S(1)} %shard_map.46) | data formatting | bytes 4194304
